TPU v7x, 32 devices: a whole 2x2x4 slice. The times are simulated.
32 devices in a mesh: row: 4 (over y, x), col: 8 (over z, core).
Axes of the slice: x: 2, y: 2, z: 4, core: 2. Of those that a mesh axis runs over, the one named last changes fastest.
Arguments:
- train_table: bfloat16 [4, 256, 262144], P('row', 'col'), may hold values from -6 to 6
- token_ids: int32 [256], replicated, may hold values from 0 to 262143
- hidden: bfloat16 [4, 256, 2560], P('row', 'col'), may hold values from -6 to 6
- w_gate: bfloat16 [4, 2560, 256], P('row'), may hold values from -0.125 to 0.125
- w_proj: bfloat16 [4, 256, 2560], P('row'), may hold values from -0.375 to 0.375
- gain: bfloat16 [4, 2560], P('row'), may hold values from 0.5 to 1.5
Outputs:
- serve_table: bfloat16 [4, 256, 262144], P(None, None, ('row', 'col'))
- update: bfloat16 [4, 256, 2560], P('row', 'col')
All inputs are finite; a program needn't handle non-finite values.
Results may differ from a plain program's by a relative error of at most 0.0048.
Values may be sent and summed in bfloat16 or wider, within the bound.
A program may use at most 256 MiB of HBM per device.

v0:
```python
import jax
import jax.numpy as jnp
from jax import lax
from jax.sharding import PartitionSpec as P


def shards(train_table, token_ids, hidden, w_gate, w_proj, gain):
    row_count = lax.axis_size("row")
    col_count = lax.axis_size("col")
    devices_all = row_count * col_count
    columns = train_table.shape[1]
    local_vocab = train_table.shape[2] // devices_all
    shaped = train_table.reshape(columns, devices_all, local_vocab)
    arrived = lax.all_to_all(shaped, ("row", "col"), split_axis=1, concat_axis=0, tiled=True)
    served = arrived.reshape(row_count, col_count * columns, local_vocab)
    picked = jnp.take(train_table[0], token_ids, axis=1)
    picked = picked.reshape(columns, col_count, picked.shape[1] // col_count)
    owned = lax.all_to_all(picked, "col", split_axis=1, concat_axis=0, tiled=True)
    owned = owned.reshape(owned.shape[0], owned.shape[2])
    emb = jnp.transpose(owned).astype(jnp.float32)
    current = hidden[0]
    gate_pre = jnp.dot(current, w_gate[0], preferred_element_type=jnp.float32)
    gated = jax.nn.gelu(gate_pre, approximate=True)
    mixed = (gated * emb).astype(jnp.bfloat16)
    projected = jnp.dot(mixed, w_proj[0], preferred_element_type=jnp.float32)
    inverse_rms = lax.rsqrt(jnp.mean(projected * projected, axis=-1, keepdims=True) + 1e-06)
    update = (projected * inverse_rms * gain[0].astype(jnp.float32)[None, :]).astype(jnp.bfloat16)
    return (served, update[None])


def solution(mesh):
    in_specs = (
        P("row", "col", None),
        P(),
        P("row", "col", None),
        P("row", None, None),
        P("row", None, None),
        P("row", None),
    )
    out_specs = (P(None, None, ("row", "col")), P("row", "col", None))
    return jax.shard_map(shards, mesh=mesh, in_specs=in_specs, out_specs=out_specs, check_vma=False)
```

profile of v0, /device:TPU:0, one launch (start us, length us, event | category | flops | bytes accessed | tf_op | source)
XLA Modules:
  0.0 482.5 jit_solution(9534343345396576181)
XLA Ops:
  0.6 0.0 copy-start
  0.6 0.8 compare_select_fusion
  1.4 0.7 compare_and_fusion
  2.1 49.1 %copy.16 = bf16[1,32,262144]{1,2,0:T(8,128)(2,1)} copy(bf16[1,32,262144]{2,1,0:T(8,128)(2,1)} %param.6) | data formatting | bytes 33554432 | tf_op args[0]
  51.2 0.1 broadcast_in_dim.19
  51.3 2.4 gather_fusion
  53.7 0.1 fusion.44
  53.8 0.7 reshape.52
  54.5 6.4 %all-to-all-start.1 = ((bf16[8,2,512]{2,1,0:T(2,128)(2,1)}), bf16[8,2,512]{2,1,0:T(2,128)(2,1)S(1)}, u32[]{:S(2)}, u32[]{:S(2)}) async-start(bf16[8,2,512]{2,1,0:T(2,128)(2,1)} %reshape.52), calls=%async_computation.1 | async-start | bytes 32768 | tf_op jit(solution)/shard_map/all_to_all | solution.py:18
  60.9 14.7 %copy.18 = bf16[4,8,32,8192]{3,2,1,0:T(8,128)(2,1)S(1)} copy(bf16[4,8,32,8192]{3,1,2,0:T(8,128)(2,1)} %bitcast.65) | data formatting | bytes 33554432
  75.6 22.2 %copy.15 = bf16[32,32,8192]{2,0,1:T(8,128)(2,1)} copy(bf16[32,32,8192]{2,1,0:T(8,128)(2,1)S(1)} %bitcast.66) | data formatting | bytes 33554432 | tf_op jit(solution)/shard_map/reshape | solution.py:13
  97.8 0.0 copy-start.3
  97.8 0.0 copy-start.1
  97.8 0.0 copy-start.2
  97.8 0.0 all-to-all-done.1
  97.8 6.2 %all-to-all-start = ((bf16[32,32,8192]{2,0,1:T(8,128)(2,1)}), bf16[32,32,8192]{2,0,1:T(8,128)(2,1)}, u32[]{:S(2)}, u32[]{:S(2)}) async-start(bf16[32,32,8192]{2,0,1:T(8,128)(2,1)} %copy.15), calls=%async_computation | async-start | bytes 33554432 | tf_op jit(solution)/shard_map/all_to_all | solution.py:14
  104.0 0.0 copy-done.3
  104.1 0.1 reshape.53
  104.2 0.1 copy.17
  104.3 0.1 reshape.40
  104.4 0.0 copy-done
  104.4 0.0 copy-done.1
  104.4 0.0 copy-done.2
  104.4 1.0 multiply_reduce_fusion
  105.4 0.8 fusion.4
  106.2 362.4 %all-to-all-done = bf16[32,32,8192]{2,0,1:T(8,128)(2,1)} async-done(((bf16[32,32,8192]{2,0,1:T(8,128)(2,1)}), bf16[32,32,8192]{2,0,1:T(8,128)(2,1)}, u32[]{:S(2)}, u32[]{:S(2)}) %all-to-all-start) | async-done | bytes 16777248 | tf_op jit(solution)/shard_map/all_to_all | solution.py:14
  468.6 14.0 %copy.20 = bf16[4,256,8192]{2,1,0:T(8,128)(2,1)} copy(bf16[4,256,8192]{2,1,0:T(8,128)(2,1)} %bitcast.2) | data formatting | bytes 33554432
  (4 shorter events, 0.1 us)
Async XLA Ops:
  0.6 103.8 %copy-start = (bf16[1,256,2560]{2,1,0:T(8,128)(2,1)S(1)}, bf16[1,256,2560]{2,1,0:T(8,128)(2,1)}, u32[]{:S(2)}) copy-start(bf16[1,256,2560]{2,1,0:T(8,128)(2,1)} %param.10) | copy-start | bytes 3932164
  54.5 43.3 %all-to-all-start.1 = ((bf16[8,2,512]{2,1,0:T(2,128)(2,1)}), bf16[8,2,512]{2,1,0:T(2,128)(2,1)S(1)}, u32[]{:S(2)}, u32[]{:S(2)}) async-start(bf16[8,2,512]{2,1,0:T(2,128)(2,1)} %reshape.52), calls=%async_computation.1 | async-start | bytes 32768 | tf_op jit(solution)/shard_map/all_to_all | solution.py:18
  97.8 6.2 %copy-start.3 = (bf16[1,2560]{1,0:T(2,128)(2,1)S(1)}, bf16[1,2560]{1,0:T(2,128)(2,1)}, u32[]{:S(2)}) copy-start(bf16[1,2560]{1,0:T(2,128)(2,1)} %param.11) | copy-start | bytes 15364
  97.8 6.6 %copy-start.1 = (bf16[1,2560,256]{2,1,0:T(8,128)(2,1)S(1)}, bf16[1,2560,256]{2,1,0:T(8,128)(2,1)}, u32[]{:S(2)}) copy-start(bf16[1,2560,256]{2,1,0:T(8,128)(2,1)} %param.9) | copy-start | bytes 3932164
  97.8 6.6 %copy-start.2 = (bf16[1,32,2560]{2,1,0:T(8,128)(2,1)S(1)}, bf16[1,32,2560]{2,1,0:T(8,128)(2,1)}, u32[]{:S(2)}) copy-start(bf16[1,32,2560]{2,1,0:T(8,128)(2,1)} %param.8) | copy-start | bytes 491524
  97.8 370.8 %all-to-all-start = ((bf16[32,32,8192]{2,0,1:T(8,128)(2,1)}), bf16[32,32,8192]{2,0,1:T(8,128)(2,1)}, u32[]{:S(2)}, u32[]{:S(2)}) async-start(bf16[32,32,8192]{2,0,1:T(8,128)(2,1)} %copy.15), calls=%async_computation | async-start | bytes 33554432 | tf_op jit(solution)/shard_map/all_to_all | solution.py:14
where the time goes:
time: 484 us; the launch traced here: 483 us
  waiting for transfers between devices  362 us (75%)
  local copies, waits for them, and re-layouts  103 us (21%)
  starting transfers between devices  12.6 us (3%)
    all_to_all x1, waiting for transfers between devices, shards(): lax.all_to_all(shaped, ('row', 'col'), split_axis=1, concat_axis=0, tiled...  362 us
    unnamed x13, local copies, waits for them, and re-layouts  78.6 us
    reshape x1, local copies, waits for them, and re-layouts, shards(): shaped = train_table.reshape(columns, devices_all, local_vocab)  22.2 us
  transfers between devices with their start and end apart: 2, of which 1 were waited for; matrix products, arithmetic and copies ran while one was open for 8% of the time, Pallas kernels for 0%

commit v1 on v0

v1 whole, which is shorter than its diff:
```python
import functools

import jax
import jax.numpy as jnp
from jax import lax
from jax.experimental import pallas as pl
from jax.experimental.pallas import tpu as pltpu
from jax.sharding import PartitionSpec as P

MESH = pl.DeviceIdType.MESH


def gather_kernel(ids_ref, table_ref, tiles_ref, sem):
    def fetch(i, carry):
        start = pl.multiple_of(lax.div(ids_ref[i], 128) * 128, 128)
        pltpu.make_async_copy(table_ref.at[0, :, pl.ds(start, 128)], tiles_ref.at[i], sem).start()
        return carry
    lax.fori_loop(0, tiles_ref.shape[0], fetch, 0, unroll=8)
    pltpu.make_async_copy(tiles_ref, tiles_ref, sem).wait()


def exchange_kernel(
    rows, cols, ids_ref, tiles_ref, table_ref, hidden_ref, w_gate_ref, w_proj_ref, gain_ref,
    served_ref, update_ref,
    own, hidden, w_gate, w_proj, gain, picked, arrived,
    send_sem, recv_sem, emb_send_sem, emb_recv_sem, local_sem,
):
    total = rows * cols
    columns = table_ref.shape[1]
    local_vocab = table_ref.shape[2] // total
    tokens = hidden_ref.shape[1]
    lanes = picked.shape[2]
    my_row, my_col = lax.axis_index("row"), lax.axis_index("col")
    me = my_row * cols + my_col
    side = 1 - 2 * (my_col // (cols // 2))

    def place(row, col):
        start = pl.multiple_of(col * columns, columns)
        return served_ref.at[row, pl.ds(start, columns), :]

    def block(rank):
        return pl.ds(pl.multiple_of(rank * local_vocab, local_vocab), local_vocab)

    loads = [
        pltpu.make_async_copy(src, dst, local_sem.at[i])
        for i, (src, dst) in enumerate((
            (hidden_ref.at[0], hidden),
            (w_gate_ref.at[0], w_gate),
            (w_proj_ref.at[0], w_proj),
            (gain_ref, gain),
            (table_ref.at[0, :, block(me)], own),
        ))
    ]
    for load in loads:
        load.start()

    def peer(k):
        row = (my_row + k % rows) % rows
        col = (my_col + side * (k // rows) + cols) % cols
        return row, col

    def send(k):
        row, col = peer(k)
        return pltpu.make_async_remote_copy(
            src_ref=table_ref.at[0, :, block(row * cols + col)],
            dst_ref=place(my_row, my_col),
            send_sem=send_sem.at[k],
            recv_sem=recv_sem.at[me],
            device_id=(row, col),
            device_id_type=MESH,
        )

    def receive(k):
        row, col = peer(k)
        return pltpu.make_async_remote_copy(
            src_ref=table_ref.at[0, :, block(row * cols + col)],
            dst_ref=place(row, col),
            send_sem=send_sem.at[k],
            recv_sem=recv_sem.at[row * cols + col],
            device_id=(row, col),
            device_id_type=MESH,
        )

    def send_emb(k):
        col = (my_col + k) % cols
        return pltpu.make_async_remote_copy(
            src_ref=picked.at[col],
            dst_ref=arrived.at[my_col],
            send_sem=emb_send_sem.at[k],
            recv_sem=emb_recv_sem.at[k],
            device_id=(my_row, col),
            device_id_type=MESH,
        )

    def receive_emb(k):
        col = (my_col + cols - k) % cols
        return pltpu.make_async_remote_copy(
            src_ref=picked.at[col],
            dst_ref=arrived.at[col],
            send_sem=emb_send_sem.at[k],
            recv_sem=emb_recv_sem.at[k],
            device_id=(my_row, col),
            device_id_type=MESH,
        )

    def each(first, last, act):
        def body(k, carry):
            act(k)
            return carry
        lax.fori_loop(first, last, body, 0)

    barrier = pltpu.get_barrier_semaphore()

    def greet(k):
        pl.semaphore_signal(barrier, inc=1, device_id=peer(k), device_id_type=MESH)

    each(1, total, greet)
    pl.semaphore_wait(barrier, total - 1)

    half = total // 2
    each(1, half, lambda k: send(k).start())

    lane = lax.broadcasted_iota(jnp.int32, (columns, 128), 1)
    spot = lax.broadcasted_iota(jnp.int32, (columns, lanes), 1)

    def pick(col):
        def body(j, gathered):
            at = col * tokens + j
            tile = tiles_ref[at].astype(jnp.float32)
            wanted = lane == lax.rem(ids_ref[at], 128)
            value = jnp.sum(jnp.where(wanted, tile, 0.0), axis=1, keepdims=True)
            return jnp.where(spot == j, value, gathered)
        gathered = lax.fori_loop(0, tokens, body, jnp.zeros((columns, lanes), jnp.float32))
        picked[col] = gathered.astype(jnp.bfloat16)

    each(0, cols, pick)

    for load in loads:
        load.wait()
    keep = pltpu.make_async_copy(own, place(my_row, my_col), local_sem.at[len(loads)])
    keep.start()
    gate_pre = jnp.dot(hidden[...], w_gate[...], preferred_element_type=jnp.float32)
    gated = jax.nn.gelu(gate_pre, approximate=True)

    each(1, cols, lambda k: send_emb(k).start())
    each(half, total, lambda k: send(k).start())

    arrived[my_col] = picked[my_col]
    each(1, cols, lambda k: receive_emb(k).wait_recv())
    flat = arrived[...].astype(jnp.float32).reshape(cols * columns, lanes)
    emb = jnp.transpose(flat)[:tokens, :]
    mixed = (gated * emb).astype(jnp.bfloat16)
    projected = jnp.dot(mixed, w_proj[...], preferred_element_type=jnp.float32)
    inverse_rms = lax.rsqrt(jnp.mean(projected * projected, axis=-1, keepdims=True) + 1e-06)
    scaled = projected * inverse_rms * gain[...].astype(jnp.float32)
    update_ref[0] = scaled.astype(jnp.bfloat16)

    each(1, cols, lambda k: send_emb(k).wait_send())
    keep.wait()
    each(1, total, lambda k: receive(k).wait_recv())
    each(1, total, lambda k: send(k).wait_send())


def shards(train_table, token_ids, hidden, w_gate, w_proj, gain):
    rows = lax.axis_size("row")
    cols = lax.axis_size("col")
    total = rows * cols
    columns, vocab = train_table.shape[1:]
    tokens, width = hidden.shape[1:]
    p_size = w_gate.shape[2]
    lanes = -(-tokens // 128) * 128
    anywhere = pl.BlockSpec(memory_space=pl.ANY)
    tiles = pl.pallas_call(
        gather_kernel,
        out_shape=jax.ShapeDtypeStruct((token_ids.shape[0], columns, 128), train_table.dtype),
        in_specs=[pl.BlockSpec(memory_space=pltpu.SMEM), anywhere],
        out_specs=pl.BlockSpec(memory_space=pltpu.VMEM),
        scratch_shapes=[pltpu.SemaphoreType.DMA],
    )(token_ids, train_table)
    served, update = pl.pallas_call(
        functools.partial(exchange_kernel, rows, cols),
        out_shape=(
            jax.ShapeDtypeStruct((rows, cols * columns, vocab // total), train_table.dtype),
            jax.ShapeDtypeStruct(hidden.shape, jnp.bfloat16),
        ),
        in_specs=[pl.BlockSpec(memory_space=pltpu.SMEM), pl.BlockSpec(memory_space=pltpu.VMEM)] + [anywhere] * 5,
        out_specs=(anywhere, pl.BlockSpec(memory_space=pltpu.VMEM)),
        scratch_shapes=[
            pltpu.VMEM((columns, vocab // total), jnp.bfloat16),
            pltpu.VMEM((tokens, width), jnp.bfloat16),
            pltpu.VMEM((width, p_size), jnp.bfloat16),
            pltpu.VMEM((p_size, width), jnp.bfloat16),
            pltpu.VMEM((1, width), jnp.bfloat16),
            pltpu.VMEM((cols, columns, lanes), jnp.bfloat16),
            pltpu.VMEM((cols, columns, lanes), jnp.bfloat16),
            pltpu.SemaphoreType.DMA((total,)),
            pltpu.SemaphoreType.DMA((total,)),
            pltpu.SemaphoreType.DMA((cols,)),
            pltpu.SemaphoreType.DMA((cols,)),
            pltpu.SemaphoreType.DMA((6,)),
        ],
        compiler_params=pltpu.CompilerParams(collective_id=0, has_side_effects=True),
    )(token_ids, tiles, train_table, hidden, w_gate, w_proj, gain)
    return (served, update)


def solution(mesh):
    in_specs = (
        P("row", "col", None),
        P(),
        P("row", "col", None),
        P("row", None, None),
        P("row", None, None),
        P("row", None),
    )
    out_specs = (P(None, None, ("row", "col")), P("row", "col", None))
    return jax.shard_map(shards, mesh=mesh, in_specs=in_specs, out_specs=out_specs, check_vma=False)
```

time: 484 us -> 454 us (0.938)
  the two profiles are of different devices: /device:TPU:0 before, /device:TPU:31 now
where the time goes in v1:
time: 454 us; the launch traced here: 453 us
  Pallas kernels  438 us (96%)
  local copies, waits for them, and re-layouts  14.7 us (3%)
    pallas_call x1, Pallas kernels, shards(): pl.pallas_call(functools.partial(exchange_kernel, rows, cols), out_shape=...  434 us
    unnamed x4, local copies, waits for them, and re-layouts  14.7 us

profile of v1, /device:TPU:31, one launch (start us, length us, event | category | flops | bytes accessed | tf_op | source)
XLA Modules:
  0.0 453.5 jit_solution(15059992301169663022)
XLA Ops:
  0.6 4.0 shard_map.77.tiles_ref
  4.7 434.2 %shard_map.78 = (bf16[4,256,8192]{2,1,0:T(8,128)(2,1)}, bf16[1,32,2560]{2,1,0:T(8,128)(2,1)}) custom-call(s32[256]{0:T(256)} %ids_ref.3, bf16[256,32,128]{2,1,0:T(8,128)(2,1)} %shard_map.77.tiles_ref, bf16[1,32,262144]{2,1,0:T(8,128)(2,1)} %table_ref.3, bf16[1,32,2560]{2,1,0:T(8,128)(2,1)} %hidden_ref.1, bf16[1,2560,256]{2,1,0:T(8,128)(2,1)} %w_gate_ref.1, ...), custom_call_target="tpu_custom_call" | custom-call | tf_op jit(solution)/shard_map/pallas_call | solution.py:180
  438.8 0.0 copy-start
  438.8 14.0 %copy.10 = bf16[4,256,8192]{2,1,0:T(8,128)(2,1)} copy(bf16[4,256,8192]{2,1,0:T(8,128)(2,1)} %get-tuple-element.4) | data formatting | bytes 33554432
  452.8 0.0 copy-done
  452.8 0.7 copy.11
Async XLA Ops:
  438.8 14.0 %copy-start = (bf16[1,32,2560]{2,1,0:T(8,128)(2,1)S(1)}, bf16[1,32,2560]{2,1,0:T(8,128)(2,1)}, u32[]{:S(2)}) copy-start(bf16[1,32,2560]{2,1,0:T(8,128)(2,1)} %get-tuple-element.5) | copy-start | bytes 491524

commit v2 on v1

--- a/solution.py
+++ b/solution.py
@@ -21,8 +21,8 @@
 
 def exchange_kernel(
     rows, cols, ids_ref, tiles_ref, table_ref, hidden_ref, w_gate_ref, w_proj_ref, gain_ref,
-    served_ref, update_ref,
-    own, hidden, w_gate, w_proj, gain, picked, arrived,
+    served_ref, update_ref, late_ref,
+    own, late, hidden, w_gate, w_proj, gain, picked, arrived,
     send_sem, recv_sem, emb_send_sem, emb_recv_sem, local_sem,
 ):
     total = rows * cols
@@ -33,6 +33,7 @@
     my_row, my_col = lax.axis_index("row"), lax.axis_index("col")
     me = my_row * cols + my_col
     side = 1 - 2 * (my_col // (cols // 2))
+    core = my_col % 2
 
     def place(row, col):
         start = pl.multiple_of(col * columns, columns)
@@ -49,12 +50,14 @@
             (w_proj_ref.at[0], w_proj),
             (gain_ref, gain),
             (table_ref.at[0, :, block(me)], own),
+            (table_ref.at[0, :, block(my_row * cols + (my_col + cols // 2) % cols)], late),
         ))
     ]
     for load in loads:
         load.start()
 
     def peer(k):
+        k = core * (total - k) + (1 - core) * k
         row = (my_row + k % rows) % rows
         col = (my_col + side * (k // rows) + cols) % cols
         return row, col
@@ -118,7 +121,9 @@
     pl.semaphore_wait(barrier, total - 1)
 
     half = total // 2
+    cut = total * 3 // 4
     each(1, half, lambda k: send(k).start())
+    each(half + 1, cut, lambda k: send(k).start())
 
     lane = lax.broadcasted_iota(jnp.int32, (columns, 128), 1)
     spot = lax.broadcasted_iota(jnp.int32, (columns, lanes), 1)
@@ -139,11 +144,13 @@
         load.wait()
     keep = pltpu.make_async_copy(own, place(my_row, my_col), local_sem.at[len(loads)])
     keep.start()
+    put = pltpu.make_async_copy(late, late_ref, local_sem.at[len(loads) + 1])
+    put.start()
     gate_pre = jnp.dot(hidden[...], w_gate[...], preferred_element_type=jnp.float32)
     gated = jax.nn.gelu(gate_pre, approximate=True)
 
     each(1, cols, lambda k: send_emb(k).start())
-    each(half, total, lambda k: send(k).start())
+    each(cut, total, lambda k: send(k).start())
 
     arrived[my_col] = picked[my_col]
     each(1, cols, lambda k: receive_emb(k).wait_recv())
@@ -157,8 +164,31 @@
 
     each(1, cols, lambda k: send_emb(k).wait_send())
     keep.wait()
-    each(1, total, lambda k: receive(k).wait_recv())
-    each(1, total, lambda k: send(k).wait_send())
+    put.wait()
+    for first, last in ((1, half), (half + 1, total)):
+        each(first, last, lambda k: receive(k).wait_recv())
+        each(first, last, lambda k: send(k).wait_send())
+
+
+def copy_kernel(served_ref, update_ref, served_out_ref, update_out_ref):
+    served_out_ref[...] = served_ref[...]
+    update_out_ref[...] = update_ref[...]
+
+
+def settle(served, update):
+    rows, depth, width = served.shape
+    step = depth // 4
+    table = pl.BlockSpec((1, step, width), lambda i, j: (i, j, 0))
+    small = pl.BlockSpec(update.shape, lambda i, j: (0, 0, 0))
+    moved = 2 * (served.size + update.size) * served.dtype.itemsize
+    return pl.pallas_call(
+        copy_kernel,
+        out_shape=tuple(jax.ShapeDtypeStruct(x.shape, x.dtype) for x in (served, update)),
+        grid=(rows, depth // step),
+        in_specs=[table, small],
+        out_specs=(table, small),
+        cost_estimate=pl.CostEstimate(flops=0, bytes_accessed=moved, transcendentals=0),
+    )(served, update)
 
 
 def shards(train_table, token_ids, hidden, w_gate, w_proj, gain):
@@ -177,15 +207,17 @@
         out_specs=pl.BlockSpec(memory_space=pltpu.VMEM),
         scratch_shapes=[pltpu.SemaphoreType.DMA],
     )(token_ids, train_table)
-    served, update = pl.pallas_call(
+    served, update, late = pl.pallas_call(
         functools.partial(exchange_kernel, rows, cols),
         out_shape=(
             jax.ShapeDtypeStruct((rows, cols * columns, vocab // total), train_table.dtype),
             jax.ShapeDtypeStruct(hidden.shape, jnp.bfloat16),
+            jax.ShapeDtypeStruct((columns, vocab // total), train_table.dtype),
         ),
         in_specs=[pl.BlockSpec(memory_space=pltpu.SMEM), pl.BlockSpec(memory_space=pltpu.VMEM)] + [anywhere] * 5,
-        out_specs=(anywhere, pl.BlockSpec(memory_space=pltpu.VMEM)),
+        out_specs=(anywhere, pl.BlockSpec(memory_space=pltpu.VMEM), anywhere),
         scratch_shapes=[
+            pltpu.VMEM((columns, vocab // total), jnp.bfloat16),
             pltpu.VMEM((columns, vocab // total), jnp.bfloat16),
             pltpu.VMEM((tokens, width), jnp.bfloat16),
             pltpu.VMEM((width, p_size), jnp.bfloat16),
@@ -197,10 +229,16 @@
             pltpu.SemaphoreType.DMA((total,)),
             pltpu.SemaphoreType.DMA((cols,)),
             pltpu.SemaphoreType.DMA((cols,)),
-            pltpu.SemaphoreType.DMA((6,)),
+            pltpu.SemaphoreType.DMA((8,)),
         ],
         compiler_params=pltpu.CompilerParams(collective_id=0, has_side_effects=True),
     )(token_ids, tiles, train_table, hidden, w_gate, w_proj, gain)
+    shift = cols // 2
+    came = lax.ppermute(late, "col", [(i, (i + shift) % cols) for i in range(cols)])
+    served, update = settle(served, update)
+    source = (lax.axis_index("col") + shift) % cols
+    spot = (lax.axis_index("row"), source * columns, 0)
+    served = lax.dynamic_update_slice(served, came[None], spot)
     return (served, update)
 
 

time: 454 us -> 384 us (0.85)
  the two profiles are of different devices: /device:TPU:31 before, /device:TPU:0 now
where the time goes in v2:
time: 384 us
  Pallas kernels  373 us (97%)
  waiting for transfers between devices  7.27 us (2%)
    pallas_call x1, Pallas kernels, shards(): pl.pallas_call(functools.partial(exchange_kernel, rows, cols), out_shape=...  352 us
    pallas_call x1, Pallas kernels, settle(): pl.pallas_call(copy_kernel, out_shape=tuple((jax.ShapeDtypeStruct(x.shape...  17.5 us
  transfers between devices with their start and end apart: 1, of which 1 were waited for; matrix products, arithmetic and copies ran while one was open for 0% of the time, Pallas kernels for 5%

profile of v2, /device:TPU:0, one launch (start us, length us, event | category | flops | bytes accessed | tf_op | source)
XLA Modules:
  0.0 383.7 jit_solution(9422981453587456588)
XLA Ops:
  0.6 4.0 %shard_map.77.tiles_ref = bf16[256,32,128]{2,1,0:T(8,128)(2,1)} custom-call(s32[256]{0:T(256)} %ids_ref.3, bf16[1,32,262144]{2,1,0:T(8,128)(2,1)} %table_ref.3), custom_call_target="tpu_custom_call" | custom-call | tf_op jit(solution)/shard_map/pallas_call | solution.py:203
  4.7 351.7 %shard_map.78 = (bf16[4,256,8192]{2,1,0:T(8,128)(2,1)}, bf16[1,32,2560]{2,1,0:T(8,128)(2,1)}, bf16[32,8192]{1,0:T(8,128)(2,1)}) custom-call(s32[256]{0:T(256)} %ids_ref.3, bf16[256,32,128]{2,1,0:T(8,128)(2,1)} %shard_map.77.tiles_ref, bf16[1,32,262144]{2,1,0:T(8,128)(2,1)} %table_ref.3, bf16[1,32,2560]{2,1,0:T(8,128)(2,1)} %hidden_ref.1, ...), custom_call_target="tpu_custom_call" | custom-call | tf_op jit(solution)/shard_map/pallas_call | solution.py:210
  356.3 1.8 collective-permute-start
  358.1 17.5 %shard_map.79 = (bf16[4,256,8192]{2,1,0:T(8,128)(2,1)}, bf16[1,32,2560]{2,1,0:T(8,128)(2,1)}) custom-call(bf16[4,256,8192]{2,1,0:T(8,128)(2,1)} %get-tuple-element.7.served_ref, bf16[1,32,2560]{2,1,0:T(8,128)(2,1)} %get-tuple-element.8.update_ref), custom_call_target="tpu_custom_call" | custom-call | bytes 33882112 | tf_op jit(solution)/shard_map/pallas_call | solution.py:184
  375.6 7.3 %collective-permute-done = bf16[32,8192]{1,0:T(8,128)(2,1)S(1)} collective-permute-done((bf16[32,8192]{1,0:T(8,128)(2,1)}, bf16[32,8192]{1,0:T(8,128)(2,1)S(1)}, u32[]{:S(2)}, u32[]{:S(2)}) %collective-permute-start) | collective-permute-done | bytes 524320 | tf_op jit(solution)/shard_map/ppermute | solution.py:237
  382.9 0.8 bitcast_dynamic-update-slice_fusion
Async XLA Ops:
  356.3 26.5 %collective-permute-start = (bf16[32,8192]{1,0:T(8,128)(2,1)}, bf16[32,8192]{1,0:T(8,128)(2,1)S(1)}, u32[]{:S(2)}, u32[]{:S(2)}) collective-permute-start(bf16[32,8192]{1,0:T(8,128)(2,1)} %get-tuple-element.10), channel_id=1, source_target_pairs={{0,4},{1,5},{2,6},{3,7},{4,0},{5,1},{6,2},{7,3},{8,12},{9,13},{10,... | collective-permute-start | bytes 1572872 | tf_op jit(solution)/shard_map/ppermute | solution.py:237
